TPU v7x, 32 devices: a whole 2x2x4 slice. The times are simulated.
32 devices in a mesh: groups: 2 (over y), expert: 4 (over x, core), etp: 4 (over z).
Axes of the slice: x: 2, y: 2, z: 4, core: 2. Of those that a mesh axis runs over, the one named last changes fastest.
Arguments:
- tokens: bfloat16 [1024, 4096], P(('groups', 'expert'), 'etp'), parts along dimension 0, may hold values from -6 to 6
- route_ids: int32 [1024, 2], P(('groups', 'expert')), parts along dimension 0, may hold values from 0 to 3, all different within a row; in each aligned block of 128 rows (0 to 127, 128 to 255, ...) at most 96 rows name the same one
- gate_weights: float32 [1024, 2], P(('groups', 'expert')), parts along dimension 0, may hold values from 0.2 to 1
- w_gate: bfloat16 [4, 4096, 14336], P('expert', None, 'etp'), may hold values from -0.09375 to 0.09375
- w_up: bfloat16 [4, 4096, 14336], P('expert', None, 'etp'), may hold values from -0.09375 to 0.09375
- w_down: bfloat16 [4, 14336, 4096], P('expert', 'etp'), may hold values from -0.0625 to 0.0625
Outputs:
- mixed: bfloat16 [1024, 4096], P(('groups', 'expert'), 'etp'), parts along dimension 0
There are 2 independent parts, one for each index of `groups`. A program takes and returns all parts, laid end to end along the dimension named above; an argument that names none is the same for every part. Nothing has to cross between parts.
Inputs may be any that keep to these rules, and one draw needn't show every extreme that they name: `route_ids`: each row names two different experts. In the rows of one index of expert (128 aligned rows), no expert is named by more than 96 rows, a bound that some block reaches.
All inputs are finite; a program needn't handle non-finite values.
Results may differ from a plain program's by a relative error of at most 0.024.
Values may be sent and summed in bfloat16 or wider, within the bound.
A program may use at most 192 MiB of HBM per device.

v0:
```python
import functools

import functools

import jax
import jax.numpy as jnp
from jax import lax
from jax.experimental import pallas as pl
from jax.experimental.pallas import tpu as pltpu
from jax.sharding import PartitionSpec as P

CAP = 96


def shards(tokens, route_ids, gate_weights, w_gate, w_up, w_down):
    cycle_size = lax.axis_size("expert")
    token_count, local_width = tokens.shape
    slot_total = cycle_size * CAP
    expert_iota = lax.broadcasted_iota(jnp.int32, (1, 1, cycle_size), 2)
    hit_mask = route_ids[:, :, None] == expert_iota
    routed = jnp.any(hit_mask, axis=1).astype(jnp.int32)
    weighting = jnp.sum(jnp.where(hit_mask, gate_weights[:, :, None], 0.0), axis=1)
    slot_index = jnp.cumsum(routed, axis=0) - 1
    expert_base = lax.broadcasted_iota(jnp.int32, (1, cycle_size), 1) * CAP
    target_slot = jnp.where(routed == 1, expert_base + slot_index, -1)
    slot_iota = lax.broadcasted_iota(jnp.int32, (1, 1, slot_total), 2)
    pick_table = target_slot[:, :, None] == slot_iota
    select_table = jnp.any(pick_table, axis=1).astype(jnp.bfloat16)
    combine_table = jnp.sum(jnp.where(pick_table, weighting[:, :, None], 0.0), axis=1)
    dispatched = jnp.dot(select_table.T, tokens, preferred_element_type=jnp.float32)
    dispatched = dispatched.astype(jnp.bfloat16).reshape(cycle_size, CAP, local_width)
    gate_local = w_gate[0]
    up_local = w_up[0]
    down_local = w_down[0]
    received = lax.all_to_all(dispatched, "expert", split_axis=0, concat_axis=0, tiled=True)
    columns_in = lax.all_gather(
        received.reshape(slot_total, local_width), "etp", axis=1, tiled=True
    )
    gate_sum = jnp.dot(columns_in, gate_local, preferred_element_type=jnp.float32)
    up_sum = jnp.dot(columns_in, up_local, preferred_element_type=jnp.float32)
    hidden = (jax.nn.silu(gate_sum) * up_sum).astype(jnp.bfloat16)
    partial_out = jnp.dot(hidden, down_local, preferred_element_type=jnp.float32).astype(
        jnp.bfloat16
    )
    finished = (
        lax.psum_scatter(partial_out, "etp", scatter_dimension=1, tiled=True)
        .astype(jnp.float32)
        .astype(jnp.bfloat16)
    )
    results = lax.all_to_all(
        finished.reshape(cycle_size, CAP, local_width),
        "expert",
        split_axis=0,
        concat_axis=0,
        tiled=True,
    )
    flat_results = results.reshape(slot_total, local_width).astype(jnp.float32)
    mixed = jnp.dot(combine_table, flat_results, precision=lax.Precision.HIGHEST)
    return mixed.astype(jnp.bfloat16)


FOUR = 4
RING_IN = 5
RING_OUT = 5
TILE_IN = 896
TILE_OUT = 256
PIECE = 512


def partner(me, step):
    low = (me % 2 + step % 2) % 2
    high = (me // 2 + step // 2) % 2
    return low + 2 * high


def layer_kernel(
    tok_ref, meta_ref, gate_hbm, up_hbm, down_hbm, out_ref,
    metas, toks, chosen, pick, comb, acc_gate, acc_up, hidden,
    ring_in, ring_out, kept, core_out, core_in, x_out, x_in, z_out, z_in,
    sem_in, sem_out, meta_s, meta_r, z_s, z_r, x_s, x_r, ca_s, ca_r, cb_s, cb_r,
    rc_s, rc_r, rx_s, rx_r, rz_s, rz_r,
):
    rows, width = tok_ref.shape
    inner = gate_hbm.shape[2]
    e = lax.axis_index("expert")
    z = lax.axis_index("etp")
    tiles_in = inner // TILE_IN
    steps_in = FOUR * tiles_in
    pieces = width // PIECE
    per_piece = PIECE // TILE_OUT
    steps_out = FOUR * width // TILE_OUT
    order_out = (2, 3, 1, 0)

    def fetch_in(t, slot):
        row = pl.multiple_of(partner(z, t // tiles_in) * width, width)
        col = pl.multiple_of((t % tiles_in) * TILE_IN, TILE_IN)
        return [
            pltpu.make_async_copy(
                hbm.at[0, pl.ds(row, width), pl.ds(col, TILE_IN)],
                ring_in.at[slot, :, pl.ds(k * TILE_IN, TILE_IN)],
                sem_in.at[slot, k],
            )
            for k, hbm in enumerate((gate_hbm, up_hbm))
        ]

    def fetch_out(u, slot):
        per_chunk = width // TILE_OUT
        index = u // per_chunk
        step = (2 + index) % FOUR * (1 - index // 2) + (3 - index) * (index // 2)
        col = partner(z, step) * width + (u % per_chunk) * TILE_OUT
        return pltpu.make_async_copy(
            down_hbm.at[0, :, pl.ds(pl.multiple_of(col, TILE_OUT), TILE_OUT)],
            ring_out.at[slot],
            sem_out.at[slot],
        )

    def send(source, target, s_sem, r_sem, axis, step):
        me = e if axis == "expert" else z
        return pltpu.make_async_remote_copy(
            src_ref=source, dst_ref=target, send_sem=s_sem, recv_sem=r_sem,
            device_id={axis: partner(me, step)},
            device_id_type=pl.DeviceIdType.MESH,
        )

    for t in range(RING_IN):
        for copy in fetch_in(t, t):
            copy.start()

    barrier = pltpu.get_barrier_semaphore()
    for step in range(1, FOUR):
        for axis, me in (("expert", e), ("etp", z)):
            pl.semaphore_signal(
                barrier, inc=1, device_id={axis: partner(me, step)},
                device_id_type=pl.DeviceIdType.MESH,
            )
    pl.semaphore_wait(barrier, 2 * (FOUR - 1))

    def block(i, j):
        return tok_ref if i == 0 and j == 0 else toks.at[i, j]

    meta_copies = [
        send(meta_ref, metas.at[j], meta_s.at[j], meta_r.at[j], "expert", j)
        for j in range(1, FOUR)
    ]
    z_copies = [None] + [
        send(tok_ref, toks.at[i, 0], z_s.at[i], z_r.at[i], "etp", i)
        for i in range(1, FOUR)
    ]
    x_copies = [
        send(block(i, 0), toks.at[i, 2], x_s.at[i], x_r.at[i], "expert", 2)
        for i in range(FOUR)
    ]
    ca_copies = [
        send(block(i, 0), toks.at[i, 1], ca_s.at[i], ca_r.at[i], "expert", 1)
        for i in range(FOUR)
    ]
    cb_copies = [
        send(toks.at[i, 2], toks.at[i, 3], cb_s.at[i], cb_r.at[i], "expert", 1)
        for i in range(FOUR)
    ]
    for copy in meta_copies:
        copy.start()
    x_copies[0].start()
    for i in range(1, FOUR):
        z_copies[i].start()
    ca_copies[0].start()

    for copy in meta_copies:
        copy.wait_recv()
    mine = e.astype(jnp.float32)
    earlier = (
        lax.broadcasted_iota(jnp.int32, (rows, rows), 0)
        < lax.broadcasted_iota(jnp.int32, (rows, rows), 1)
    ).astype(jnp.bfloat16)
    slot_row = lax.broadcasted_iota(jnp.int32, (rows, rows), 0).astype(jnp.float32)
    for j in range(FOUR):
        meta = meta_ref[...] if j == 0 else metas[j]
        first = meta[0:1, :] == mine
        second = meta[1:2, :] == mine
        routed = jnp.where(first, 1.0, 0.0) + jnp.where(second, 1.0, 0.0)
        weight = jnp.where(first, meta[2:3, :], 0.0) + jnp.where(second, meta[3:4, :], 0.0)
        slot = jnp.dot(
            jnp.broadcast_to(routed, (16, rows)).astype(jnp.bfloat16), earlier,
            preferred_element_type=jnp.float32,
        )[0:1, :]
        slot = jnp.where(routed > 0.5, slot, -1.0)
        hit = slot_row == slot
        pick[j] = jnp.where(hit, 1.0, 0.0).astype(jnp.bfloat16)
        comb[j] = jnp.where(hit, weight, 0.0).T.astype(jnp.bfloat16)

    def pass_on(i):
        z_copies[i].wait_recv()
        x_copies[i].start()
        ca_copies[i].start()

    def pass_over(i):
        x_copies[i].wait_recv()
        cb_copies[i].start()

    pass_on(1)
    pass_over(0)
    for i in range(FOUR):
        if i == FOUR - 1:
            for u in range(RING_OUT):
                fetch_out(u, u).start()
        ca_copies[i].wait_recv()
        cb_copies[i].wait_recv()
        for j in range(FOUR):
            chosen[pl.ds(j * CAP, CAP), :] = jnp.dot(
                pick[j, 0:CAP, :], block(i, j)[...], preferred_element_type=jnp.float32
            ).astype(jnp.bfloat16)

        def in_step(n, carry, i=i):
            if i + 2 < FOUR:
                pl.when(n == tiles_in // 2)(functools.partial(pass_on, i + 2))
            if i + 1 < FOUR:
                pl.when(n == tiles_in - 1)(functools.partial(pass_over, i + 1))
            t = i * tiles_in + n
            slot = lax.rem(t, RING_IN)
            for copy in fetch_in(t, slot):
                copy.wait()
            col = pl.ds(pl.multiple_of(n * TILE_IN, TILE_IN), TILE_IN)
            both = jnp.dot(chosen[...], ring_in[slot], preferred_element_type=jnp.float32)
            gate, up = both[:, :TILE_IN], both[:, TILE_IN:]
            if i > 0:
                gate = gate + acc_gate[:, col]
                up = up + acc_up[:, col]
            if i < FOUR - 1:
                acc_gate[:, col] = gate
                acc_up[:, col] = up
            else:
                hidden[:, col] = (gate / (1.0 + jnp.exp(-gate)) * up).astype(jnp.bfloat16)

            @pl.when(t + RING_IN < steps_in)
            def _():
                for copy in fetch_in(t + RING_IN, slot):
                    copy.start()

            return carry

        lax.fori_loop(0, tiles_in, in_step, 0)

    total = FOUR * pieces
    core_copies = [
        send(core_out.at[s], core_in.at[s], rc_s.at[s], rc_r.at[s], "expert", 1)
        for s in range(total)
    ]
    rx_copies = [
        send(x_out.at[s], x_in.at[s], rx_s.at[s], rx_r.at[s], "expert", 2)
        for s in range(total)
    ]
    rz_copies = [
        send(z_out.at[s], z_in.at[s], rz_s.at[s], rz_r.at[s], "etp", order_out[s // pieces])
        for s in range(total - pieces)
    ]

    def x_stage(s):
        core_copies[s].wait_recv()
        x_out[s] = (kept[s, 1] + core_in[s, 1].astype(jnp.float32)).astype(jnp.bfloat16)
        rx_copies[s].start()

    def z_stage(s):
        rx_copies[s].wait_recv()
        both = kept[s, 0] + core_in[s, 0].astype(jnp.float32) + x_in[s].astype(jnp.float32)
        if s < total - pieces:
            z_out[s] = both.astype(jnp.bfloat16)
            rz_copies[s].start()
        else:
            kept[s, 0] = both

    def down_piece(s):
        def out_step(q, carry):
            if s >= 1:
                pl.when(q == 1)(functools.partial(x_stage, s - 1))
            u = s * per_piece + q
            slot = lax.rem(u, RING_OUT)
            fetch_out(u, slot).wait()
            part = jnp.dot(
                hidden[...], ring_out[slot], preferred_element_type=jnp.float32
            ).astype(jnp.bfloat16)
            col = pl.ds(pl.multiple_of(q * TILE_OUT, TILE_OUT), TILE_OUT)
            for j in range(FOUR):
                share = jnp.dot(
                    comb[j, :, 0:CAP], part[j * CAP:(j + 1) * CAP, :],
                    preferred_element_type=jnp.float32,
                )
                if j % 2 == 0:
                    kept[s, j // 2, :, col] = share
                else:
                    core_out[s, j // 2, :, col] = share.astype(jnp.bfloat16)

            @pl.when(u + RING_OUT < steps_out)
            def _():
                fetch_out(u + RING_OUT, slot).start()

            return carry

        lax.fori_loop(0, per_piece, out_step, 0)
        core_copies[s].start()

    LAG = 3
    for s in range(total):
        down_piece(s)
        if s >= LAG:
            z_stage(s - LAG)
    x_stage(total - 1)
    for s in range(total - LAG, total):
        z_stage(s)
    for h in range(pieces):
        value = kept[total - pieces + h, 0]
        for index in range(FOUR - 1):
            s = index * pieces + h
            rz_copies[s].wait_recv()
            value = value + z_in[s].astype(jnp.float32)
        out_ref[:, h * PIECE:(h + 1) * PIECE] = value.astype(jnp.bfloat16)
    for copy in (
        meta_copies + z_copies[1:] + x_copies + ca_copies + cb_copies
        + core_copies + rx_copies + rz_copies
    ):
        copy.wait_send()


def fused(tokens, route_ids, gate_weights, w_gate, w_up, w_down):
    rows, width = tokens.shape
    inner = w_gate.shape[2]
    slots = FOUR * CAP
    total = FOUR * width // PIECE
    meta = jnp.concatenate(
        [route_ids.T.astype(jnp.float32), gate_weights.T, jnp.zeros((4, rows), jnp.float32)], axis=0
    )
    bf, f32 = jnp.bfloat16, jnp.float32
    dma = pltpu.SemaphoreType.DMA
    vmem = pl.BlockSpec(memory_space=pltpu.VMEM)
    hbm = pl.BlockSpec(memory_space=pl.ANY)
    return pl.pallas_call(
        layer_kernel,
        out_shape=jax.ShapeDtypeStruct((rows, width), bf),
        in_specs=[vmem, vmem, hbm, hbm, hbm],
        out_specs=vmem,
        scratch_shapes=[
            pltpu.VMEM((FOUR, 8, rows), f32),
            pltpu.VMEM((FOUR, FOUR, rows, width), bf),
            pltpu.VMEM((slots, width), bf),
            pltpu.VMEM((FOUR, rows, rows), bf),
            pltpu.VMEM((FOUR, rows, rows), bf),
            pltpu.VMEM((slots, inner), f32),
            pltpu.VMEM((slots, inner), f32),
            pltpu.VMEM((slots, inner), bf),
            pltpu.VMEM((RING_IN, width, 2 * TILE_IN), bf),
            pltpu.VMEM((RING_OUT, inner, TILE_OUT), bf),
            pltpu.VMEM((total, 2, rows, PIECE), f32),
            pltpu.VMEM((total, 2, rows, PIECE), bf),
            pltpu.VMEM((total, 2, rows, PIECE), bf),
            pltpu.VMEM((total, rows, PIECE), bf),
            pltpu.VMEM((total, rows, PIECE), bf),
            pltpu.VMEM((total, rows, PIECE), bf),
            pltpu.VMEM((total, rows, PIECE), bf),
            dma((RING_IN, 2)), dma((RING_OUT,)),
            dma((FOUR,)), dma((FOUR,)), dma((FOUR,)), dma((FOUR,)),
            dma((FOUR,)), dma((FOUR,)), dma((FOUR,)), dma((FOUR,)),
            dma((FOUR,)), dma((FOUR,)),
            dma((total,)), dma((total,)), dma((total,)), dma((total,)),
            dma((total,)), dma((total,)),
        ],
        compiler_params=pltpu.CompilerParams(
            collective_id=0, has_side_effects=True, vmem_limit_bytes=67043328
        ),
    )(tokens, meta, w_gate, w_up, w_down)


def pick_body(tokens, route_ids, gate_weights, w_gate, w_up, w_down):
    square = lax.axis_size("expert") == FOUR and lax.axis_size("etp") == FOUR
    whole = tokens.shape[1] % PIECE == 0 and w_gate.shape[2] % TILE_IN == 0
    lanes = tokens.shape[0] == 128 and w_gate.shape[2] // TILE_IN * FOUR >= RING_IN
    body = fused if square and whole and lanes else shards
    return body(tokens, route_ids, gate_weights, w_gate, w_up, w_down)


def solution(mesh):
    return jax.shard_map(
        pick_body,
        mesh=mesh,
        in_specs=(
            P(("groups", "expert"), "etp"),
            P(("groups", "expert"), None),
            P(("groups", "expert"), None),
            P("expert", None, "etp"),
            P("expert", None, "etp"),
            P("expert", "etp", None),
        ),
        out_specs=P(("groups", "expert"), "etp"),
        check_vma=False,
    )
```

profile of v0, /device:TPU:0, one launch (start us, length us, event | category | flops | bytes accessed | tf_op | source)
XLA Modules:
  0.0 86.9 jit_solution(7534807957996937842)
XLA Ops:
  0.0 0.1 pad.2.clone
  0.1 0.7 convert_bitcast_fusion
  0.8 1.3 %maximum_maximum_fusion.meta_ref = f32[8,128]{1,0:T(8,128)} fusion(f32[2,128]{1,0:T(2,128)} %bitcast.3, f32[2,128]{1,0:T(2,128)S(1)} %convert_bitcast_fusion, f32[8]{0:T(128)S(1)} %pad.2.clone), kind=kLoop, calls=%fused_computation | loop fusion | flops 2048 | bytes 6176 | tf_op jit(solution)/shard_map/concatenate | solution.py:328
  2.1 83.1 %shard_map.64 = bf16[128,1024]{1,0:T(8,128)(2,1)} custom-call(bf16[128,1024]{1,0:T(8,128)(2,1)} %tok_ref.1, f32[8,128]{1,0:T(8,128)} %maximum_maximum_fusion.meta_ref, bf16[1,4096,3584]{2,1,0:T(8,128)(2,1)} %gate_hbm.1, bf16[1,4096,3584]{2,1,0:T(8,128)(2,1)} %up_hbm.1, bf16[1,3584,4096]{2,1,0:T(8,128)(2,1)} %down_hbm.1), custom_call_target="tpu_custom_call" | custom-call | tf_op jit(solution)/shard_map/pallas_call | solution.py:335
  85.2 1.7 %copy.8 = bf16[128,1024]{1,0:T(8,128)(2,1)} copy(bf16[128,1024]{1,0:T(8,128)(2,1)} %shard_map.64) | data formatting | bytes 524288
  (1 shorter events, 0.0 us)
where the time goes:
time: 87.1 us; the launch traced here: 86.9 us
  Pallas kernels  83.1 us (95%)
  other arithmetic  2.02 us (2%)
  local copies, waits for them, and re-layouts  1.75 us (2%)
    pallas_call x1, Pallas kernels, fused(): pl.pallas_call(layer_kernel, out_shape=jax.ShapeDtypeStruct((rows, width)...  83.1 us

commit v1 on v0

v1 whole, which is shorter than its diff:
```python
import functools

import jax
import jax.numpy as jnp
from jax import lax
from jax.experimental import pallas as pl
from jax.experimental.pallas import tpu as pltpu
from jax.sharding import PartitionSpec as P

CAP = 96


def shards(tokens, route_ids, gate_weights, w_gate, w_up, w_down):
    cycle_size = lax.axis_size("expert")
    token_count, local_width = tokens.shape
    slot_total = cycle_size * CAP
    expert_iota = lax.broadcasted_iota(jnp.int32, (1, 1, cycle_size), 2)
    hit_mask = route_ids[:, :, None] == expert_iota
    routed = jnp.any(hit_mask, axis=1).astype(jnp.int32)
    weighting = jnp.sum(jnp.where(hit_mask, gate_weights[:, :, None], 0.0), axis=1)
    slot_index = jnp.cumsum(routed, axis=0) - 1
    expert_base = lax.broadcasted_iota(jnp.int32, (1, cycle_size), 1) * CAP
    target_slot = jnp.where(routed == 1, expert_base + slot_index, -1)
    slot_iota = lax.broadcasted_iota(jnp.int32, (1, 1, slot_total), 2)
    pick_table = target_slot[:, :, None] == slot_iota
    select_table = jnp.any(pick_table, axis=1).astype(jnp.bfloat16)
    combine_table = jnp.sum(jnp.where(pick_table, weighting[:, :, None], 0.0), axis=1)
    dispatched = jnp.dot(select_table.T, tokens, preferred_element_type=jnp.float32)
    dispatched = dispatched.astype(jnp.bfloat16).reshape(cycle_size, CAP, local_width)
    gate_local = w_gate[0]
    up_local = w_up[0]
    down_local = w_down[0]
    received = lax.all_to_all(dispatched, "expert", split_axis=0, concat_axis=0, tiled=True)
    columns_in = lax.all_gather(
        received.reshape(slot_total, local_width), "etp", axis=1, tiled=True
    )
    gate_sum = jnp.dot(columns_in, gate_local, preferred_element_type=jnp.float32)
    up_sum = jnp.dot(columns_in, up_local, preferred_element_type=jnp.float32)
    hidden = (jax.nn.silu(gate_sum) * up_sum).astype(jnp.bfloat16)
    partial_out = jnp.dot(hidden, down_local, preferred_element_type=jnp.float32).astype(
        jnp.bfloat16
    )
    finished = (
        lax.psum_scatter(partial_out, "etp", scatter_dimension=1, tiled=True)
        .astype(jnp.float32)
        .astype(jnp.bfloat16)
    )
    results = lax.all_to_all(
        finished.reshape(cycle_size, CAP, local_width),
        "expert",
        split_axis=0,
        concat_axis=0,
        tiled=True,
    )
    flat_results = results.reshape(slot_total, local_width).astype(jnp.float32)
    mixed = jnp.dot(combine_table, flat_results, precision=lax.Precision.HIGHEST)
    return mixed.astype(jnp.bfloat16)


FOUR = 4
HALVES = 2
RING_IN = 5
RING_OUT = 3
BLOCK = 256
LEAD = 4
TARGETS = (0, 0, 0, 1, 0, 1, 2, 1, 2, 1, 2, 2, 3, 3, 3, 3)


def partner(me, step):
    low = (me % 2 + step % 2) % 2
    high = (me // 2 + step // 2) % 2
    return low + 2 * high


def layer_kernel(
    tok_hbm, route_hbm, weight_hbm, gate_hbm, up_hbm, down_hbm, out_hbm,
    routes, weights, toks, chosen, pick, comb, acc_gate, acc_up, hidden,
    ring_in, ring_out, kept, core_out, core_in, x_out, x_in, z_out, z_in, out_vmem,
    sem_in, sem_out, sem_own, sem_put, meta_s, meta_r, z_s, z_r, zf_s,
    x_s, x_r, ca_s, ca_r, cb_s, cb_r, rc_s, rc_r, rx_s, rx_r, rz_s, rz_r,
):
    rows, width = tok_hbm.shape
    inner = gate_hbm.shape[2]
    e = lax.axis_index("expert")
    z = lax.axis_index("etp")
    middle = (z + 1) // 2 % 2
    sub = width // HALVES
    tile = inner // HALVES
    subs = FOUR * HALVES
    steps_in = subs * HALVES
    units = len(TARGETS)
    slabs = units // 2
    rank = [TARGETS[:i].count(TARGETS[i]) for i in range(units)]
    place = {(TARGETS[i], rank[i]): i for i in range(units)}

    def origin(p):
        return partner(z, p + middle * (p // 2) * (1 - 2 * (p % 2)))

    def fetch_in(t, slot):
        k = t // HALVES
        row = pl.multiple_of(origin(k // HALVES) * width + k % HALVES * sub, sub)
        col = pl.multiple_of(t % HALVES * tile, tile)
        return [
            pltpu.make_async_copy(
                hbm.at[0, pl.ds(row, sub), pl.ds(col, tile)],
                ring_in.at[slot, :, pl.ds(m * tile, tile)],
                sem_in.at[slot, m],
            )
            for m, hbm in enumerate((gate_hbm, up_hbm))
        ]

    def fetch_out(u):
        return [
            pltpu.make_async_copy(
                down_hbm.at[0, :, pl.ds(
                    pl.multiple_of(
                        partner(z, FOUR - 1 - TARGETS[i]) * width + rank[i] * BLOCK, BLOCK
                    ), BLOCK
                )],
                ring_out.at[u % RING_OUT, :, pl.ds(i % 2 * BLOCK, BLOCK)],
                sem_out.at[u % RING_OUT, i % 2],
            )
            for i in (2 * u, 2 * u + 1)
        ]

    def send(source, target, s_sem, r_sem, axis, step):
        me = e if axis == "expert" else z
        return pltpu.make_async_remote_copy(
            src_ref=source, dst_ref=target, send_sem=s_sem, recv_sem=r_sem,
            device_id={axis: partner(me, step)},
            device_id_type=pl.DeviceIdType.MESH,
        )

    barrier = pltpu.get_barrier_semaphore()

    def greet(axis, me, step):
        pl.semaphore_signal(
            barrier, inc=1, device_id={axis: partner(me, step)},
            device_id_type=pl.DeviceIdType.MESH,
        )

    greet("etp", z, 2)
    pl.when(middle == 1)(lambda: greet("etp", z, 3))
    greet("etp", z, 1)
    for step in (3, 2, 1):
        greet("expert", e, step)

    own = [
        pltpu.make_async_copy(route_hbm, routes.at[0], sem_own.at[0]),
        pltpu.make_async_copy(weight_hbm, weights.at[0], sem_own.at[1]),
    ] + [
        pltpu.make_async_copy(
            tok_hbm.at[:, pl.ds(h * sub, sub)], toks.at[0, 0, h], sem_own.at[2 + h]
        )
        for h in range(HALVES)
    ]
    for copy in own:
        copy.start()
    for copy in own:
        copy.wait()
    for t in range(RING_IN):
        for copy in fetch_in(t, t):
            copy.start()
    pl.semaphore_wait(barrier, FOUR + 1 + middle)

    meta_copies = [
        send(
            held.at[0], held.at[j], meta_s.at[m, j], meta_r.at[m, j], "expert", j,
        )
        for j in (2, 3, 1)
        for m, held in enumerate((routes, weights))
    ]
    near_copies = [
        send(toks.at[0, 0, h], toks.at[1, 0, h], z_s.at[0, h], z_r.at[1, h], "etp", 1)
        for h in range(HALVES)
    ]
    far_copies = [
        send(
            toks.at[0, 0, h], toks.at[3 - middle, 0, h], z_s.at[1, h],
            z_r.at[3 - middle, h], "etp", 2 + middle,
        )
        for h in range(HALVES)
    ]
    z_copies, forward, x_copies, ca_copies, cb_copies = [], [], [], [], []
    for k in range(subs):
        p, h = k // HALVES, k % HALVES
        mine = toks.at[p, 0, h]
        z_copies.append(send(mine, mine, zf_s.at[p, h], z_r.at[p, h], "etp", 1))
        x_copies.append(
            send(mine, toks.at[p, 2, h], x_s.at[k], x_r.at[k], "expert", 2)
        )
        ca_copies.append(
            send(mine, toks.at[p, 1, h], ca_s.at[k], ca_r.at[k], "expert", 1)
        )
        cb_copies.append(
            send(toks.at[p, 2, h], toks.at[p, 3, h], cb_s.at[k], cb_r.at[k], "expert", 1)
        )
    for copy in meta_copies:
        copy.start()
    for h in range(HALVES):
        x_copies[h].start()
        near_copies[h].start()
    for h in range(HALVES):
        far_copies[h].start()
        ca_copies[h].start()

    for copy in meta_copies:
        copy.wait_recv()
    earlier = (
        lax.broadcasted_iota(jnp.int32, (rows, rows), 0)
        < lax.broadcasted_iota(jnp.int32, (rows, rows), 1)
    ).astype(jnp.bfloat16)
    slot_row = lax.broadcasted_iota(jnp.int32, (rows, rows), 0).astype(jnp.float32)
    for j in range(FOUR):
        route, weigh = routes[j], weights[j]
        first = route[0:1, :] == e
        second = route[1:2, :] == e
        routed = jnp.where(first, 1.0, 0.0) + jnp.where(second, 1.0, 0.0)
        weight = jnp.where(first, weigh[0:1, :], 0.0) + jnp.where(second, weigh[1:2, :], 0.0)
        slot = jnp.dot(
            jnp.broadcast_to(routed, (16, rows)).astype(jnp.bfloat16), earlier,
            preferred_element_type=jnp.float32,
        )[0:1, :]
        slot = jnp.where(routed > 0.5, slot, -1.0)
        hit = slot_row == slot
        pick[j] = jnp.where(hit, 1.0, 0.0).astype(jnp.bfloat16)
        comb[j] = jnp.where(hit, weight, 0.0).T.astype(jnp.bfloat16)

    def pass_over(k):
        if k < subs:
            x_copies[k].wait_recv()
            cb_copies[k].start()

    def pass_on(k):
        if k < subs:
            if k < 2 * HALVES:
                z_copies[k].wait_recv()
            else:
                pl.when(middle == 0)(z_copies[k].wait_recv)
            x_copies[k].start()
            ca_copies[k].start()

    def pass_out(k):
        if k < subs:

            @pl.when(middle == 1)
            def _():
                z_copies[k].wait_recv()
                z_copies[k].start()

    def poll(k):
        pass_over(k)
        pass_on(k + HALVES)
        pass_out(k + 2 * HALVES)

    poll(0)
    for k in range(subs):
        p, h = k // HALVES, k % HALVES
        ca_copies[k].wait_recv()
        cb_copies[k].wait_recv()
        for j in range(FOUR):
            chosen[pl.ds(j * CAP, CAP), :] = jnp.dot(
                pick[j, 0:CAP, :], toks[p, j, h], preferred_element_type=jnp.float32
            ).astype(jnp.bfloat16)

        if k == subs - 1:
            for u in range(RING_OUT):
                for copy in fetch_out(u):
                    copy.start()

        def in_step(n, carry, k=k):
            if k + 1 < subs:
                pl.when(n == 1)(functools.partial(poll, k + 1))
            t = k * HALVES + n
            slot = lax.rem(t, RING_IN)
            for copy in fetch_in(t, slot):
                copy.wait()
            col = pl.ds(pl.multiple_of(n * tile, tile), tile)
            both = jnp.dot(chosen[...], ring_in[slot], preferred_element_type=jnp.float32)
            gate, up = both[:, :tile], both[:, tile:]
            if k > 0:
                gate = gate + acc_gate[:, col]
                up = up + acc_up[:, col]
            if k < subs - 1:
                acc_gate[:, col] = gate
                acc_up[:, col] = up
            else:
                hidden[:, col] = (gate / (1.0 + jnp.exp(-gate)) * up).astype(jnp.bfloat16)

            @pl.when(t + RING_IN < steps_in)
            def _():
                for copy in fetch_in(t + RING_IN, slot):
                    copy.start()

            return carry

        lax.fori_loop(0, HALVES, in_step, 0)

    core_copies = [
        send(
            core_out.at[pl.ds(2 * u, 2)], core_in.at[pl.ds(2 * u, 2)],
            rc_s.at[u], rc_r.at[u], "expert", 1,
        )
        for u in range(slabs)
    ]
    rx_copies = [
        send(x_out.at[i], x_in.at[i], rx_s.at[i], rx_r.at[i], "expert", 2)
        for i in range(units)
    ]
    rz_copies = [
        send(z_out.at[i], z_in.at[i], rz_s.at[i], rz_r.at[i], "etp", (1, 2, 1)[TARGETS[i]])
        for i in range(units) if TARGETS[i] < FOUR - 1
    ]
    outs = [
        pltpu.make_async_copy(
            out_vmem.at[q], out_hbm.at[:, pl.ds(q * BLOCK, BLOCK)], sem_put.at[q]
        )
        for q in range(width // BLOCK)
    ]

    def x_stage(u):
        core_copies[u].wait_recv()
        for i in (2 * u, 2 * u + 1):
            x_out[i] = (kept[i, 1] + core_in[i, 1].astype(jnp.float32)).astype(jnp.bfloat16)
            rx_copies[i].start()

    def z_stage(i):
        q = rank[i]
        adds = {1: (0,), 3: (2, 1)}.get(TARGETS[i], ())
        rx_copies[i].wait_recv()
        both = kept[i, 0] + core_in[i, 0].astype(jnp.float32) + x_in[i].astype(jnp.float32)
        for target in adds:
            rz_copies[place[target, q]].wait_recv()
            both = both + z_in[place[target, q]].astype(jnp.float32)
        if TARGETS[i] < FOUR - 1:
            z_out[i] = both.astype(jnp.bfloat16)
            rz_copies[i].start()
        else:
            out_vmem[q] = both.astype(jnp.bfloat16)
            outs[q].start()

    def down_slab(u):
        for copy in fetch_out(u):
            copy.wait()
        part = jnp.dot(
            hidden[...], ring_out[u % RING_OUT], preferred_element_type=jnp.float32
        ).astype(jnp.bfloat16)
        for j in range(FOUR):
            share = jnp.dot(
                comb[j, :, 0:CAP], part[j * CAP:(j + 1) * CAP, :],
                preferred_element_type=jnp.float32,
            )
            for m in range(2):
                piece = share[:, m * BLOCK:(m + 1) * BLOCK]
                if j % 2 == 0:
                    kept[2 * u + m, j // 2] = piece
                else:
                    core_out[2 * u + m, j // 2] = piece.astype(jnp.bfloat16)
        core_copies[u].start()
        if u + RING_OUT < slabs:
            for copy in fetch_out(u + RING_OUT):
                copy.start()

    late, sent = 0, 0
    for u in range(slabs):
        down_slab(u)
        while sent < u or sent == u < 2:
            x_stage(sent)
            sent += 1
        while 2 * sent - late > LEAD:
            z_stage(late)
            late += 1
    x_stage(slabs - 1)
    for i in range(late, units):
        z_stage(i)
    for copy in outs:
        copy.wait()

    @pl.when(middle == 1)
    def _():
        for copy in z_copies[2 * HALVES:]:
            copy.wait_send()

    for copy in (
        meta_copies + near_copies + far_copies + x_copies + ca_copies + cb_copies
        + core_copies + rx_copies + rz_copies
    ):
        copy.wait_send()


def fused(tokens, route_ids, gate_weights, w_gate, w_up, w_down):
    rows, width = tokens.shape
    inner = w_gate.shape[2]
    slots = FOUR * CAP
    units, subs = len(TARGETS), FOUR * HALVES
    bf, f32 = jnp.bfloat16, jnp.float32
    dma = pltpu.SemaphoreType.DMA
    hbm = pl.BlockSpec(memory_space=pl.ANY)
    return pl.pallas_call(
        layer_kernel,
        out_shape=jax.ShapeDtypeStruct((rows, width), bf),
        in_specs=[hbm] * 6,
        out_specs=hbm,
        scratch_shapes=[
            pltpu.VMEM((FOUR, 2, rows), jnp.int32),
            pltpu.VMEM((FOUR, 2, rows), f32),
            pltpu.VMEM((FOUR, FOUR, HALVES, rows, width // HALVES), bf),
            pltpu.VMEM((slots, width // HALVES), bf),
            pltpu.VMEM((FOUR, rows, rows), bf),
            pltpu.VMEM((FOUR, rows, rows), bf),
            pltpu.VMEM((slots, inner), f32),
            pltpu.VMEM((slots, inner), f32),
            pltpu.VMEM((slots, inner), bf),
            pltpu.VMEM((RING_IN, width // HALVES, inner), bf),
            pltpu.VMEM((RING_OUT, inner, 2 * BLOCK), bf),
            pltpu.VMEM((units, 2, rows, BLOCK), f32),
            pltpu.VMEM((units, 2, rows, BLOCK), bf),
            pltpu.VMEM((units, 2, rows, BLOCK), bf),
            pltpu.VMEM((units, rows, BLOCK), bf),
            pltpu.VMEM((units, rows, BLOCK), bf),
            pltpu.VMEM((units, rows, BLOCK), bf),
            pltpu.VMEM((units, rows, BLOCK), bf),
            pltpu.VMEM((width // BLOCK, rows, BLOCK), bf),
            dma((RING_IN, 2)), dma((RING_OUT, 2)), dma((2 + HALVES,)), dma((width // BLOCK,)),
            dma((2, FOUR)), dma((2, FOUR)),
            dma((2, HALVES)), dma((FOUR, HALVES)), dma((FOUR, HALVES)),
            dma((subs,)), dma((subs,)), dma((subs,)), dma((subs,)),
            dma((subs,)), dma((subs,)),
            dma((units // 2,)), dma((units // 2,)), dma((units,)), dma((units,)),
            dma((units,)), dma((units,)),
        ],
        compiler_params=pltpu.CompilerParams(
            collective_id=0, has_side_effects=True, vmem_limit_bytes=67043328
        ),
    )(tokens, route_ids.T, gate_weights.T, w_gate, w_up, w_down)


def pick_body(tokens, route_ids, gate_weights, w_gate, w_up, w_down):
    square = lax.axis_size("expert") == FOUR and lax.axis_size("etp") == FOUR
    whole = tokens.shape == (128, len(TARGETS) * BLOCK // FOUR)
    lanes = w_gate.shape[2] % (HALVES * 128) == 0
    body = fused if square and whole and lanes else shards
    return body(tokens, route_ids, gate_weights, w_gate, w_up, w_down)


def solution(mesh):
    return jax.shard_map(
        pick_body,
        mesh=mesh,
        in_specs=(
            P(("groups", "expert"), "etp"),
            P(("groups", "expert"), None),
            P(("groups", "expert"), None),
            P("expert", None, "etp"),
            P("expert", None, "etp"),
            P("expert", "etp", None),
        ),
        out_specs=P(("groups", "expert"), "etp"),
        check_vma=False,
    )
```

time: 87.1 us -> 75.3 us (0.86)
  Pallas kernels: 83.1 us -> 72.8 us
  other arithmetic: 2.02 us -> 0 us
    pallas_call x1, Pallas kernels: 83.1 us -> 72.8 us  [fused(): pl.pallas_call(layer_kernel, out_shape=jax.ShapeDtypeStruct((rows, width)...]
    concatenate x1 -> x0, other arithmetic: 1.34 us -> none  [fused(): jnp.concatenate([route_ids.T.astype(jnp.float32), gate_weights.T, jnp.zer...]
where the time goes in v1:
time: 75.3 us; the launch traced here: 74.5 us
  Pallas kernels  72.8 us (97%)
  local copies, waits for them, and re-layouts  1.67 us (2%)
    pallas_call x1, Pallas kernels, fused(): pl.pallas_call(layer_kernel, out_shape=jax.ShapeDtypeStruct((rows, width)...  72.8 us
    unnamed x1, local copies, waits for them, and re-layouts  1.67 us

profile of v1, /device:TPU:0, one launch (start us, length us, event | category | flops | bytes accessed | tf_op | source)
XLA Modules:
  0.0 74.5 jit_solution(102824655610193241)
XLA Ops:
  0.0 72.8 %shard_map.64 = bf16[128,1024]{1,0:T(8,128)(2,1)} custom-call(bf16[128,1024]{1,0:T(8,128)(2,1)} %tok_hbm.1, s32[2,128]{1,0:T(2,128)} %bitcast.2, f32[2,128]{1,0:T(2,128)} %bitcast.3, bf16[1,4096,3584]{2,1,0:T(8,128)(2,1)} %gate_hbm.1, bf16[1,4096,3584]{2,1,0:T(8,128)(2,1)} %up_hbm.1, bf16[1,3584,4096]{2,1,0:T(8,128)(2,1)} %down_hbm.1), custom_call_target="tpu_custom_call" | custom-call | tf_op jit(solution)/shard_map/pallas_call | solution.py:399
  72.8 1.7 %copy.8 = bf16[128,1024]{1,0:T(8,128)(2,1)} copy(bf16[128,1024]{1,0:T(8,128)(2,1)} %shard_map.64) | data formatting | bytes 524288

commit v2 on v1

v2 whole, which is shorter than its diff:
```python
import functools

import jax
import jax.numpy as jnp
from jax import lax
from jax.experimental import pallas as pl
from jax.experimental.pallas import tpu as pltpu
from jax.sharding import PartitionSpec as P

CAP = 96


def shards(tokens, route_ids, gate_weights, w_gate, w_up, w_down):
    cycle_size = lax.axis_size("expert")
    token_count, local_width = tokens.shape
    slot_total = cycle_size * CAP
    expert_iota = lax.broadcasted_iota(jnp.int32, (1, 1, cycle_size), 2)
    hit_mask = route_ids[:, :, None] == expert_iota
    routed = jnp.any(hit_mask, axis=1).astype(jnp.int32)
    weighting = jnp.sum(jnp.where(hit_mask, gate_weights[:, :, None], 0.0), axis=1)
    slot_index = jnp.cumsum(routed, axis=0) - 1
    expert_base = lax.broadcasted_iota(jnp.int32, (1, cycle_size), 1) * CAP
    target_slot = jnp.where(routed == 1, expert_base + slot_index, -1)
    slot_iota = lax.broadcasted_iota(jnp.int32, (1, 1, slot_total), 2)
    pick_table = target_slot[:, :, None] == slot_iota
    select_table = jnp.any(pick_table, axis=1).astype(jnp.bfloat16)
    combine_table = jnp.sum(jnp.where(pick_table, weighting[:, :, None], 0.0), axis=1)
    dispatched = jnp.dot(select_table.T, tokens, preferred_element_type=jnp.float32)
    dispatched = dispatched.astype(jnp.bfloat16).reshape(cycle_size, CAP, local_width)
    gate_local = w_gate[0]
    up_local = w_up[0]
    down_local = w_down[0]
    received = lax.all_to_all(dispatched, "expert", split_axis=0, concat_axis=0, tiled=True)
    columns_in = lax.all_gather(
        received.reshape(slot_total, local_width), "etp", axis=1, tiled=True
    )
    gate_sum = jnp.dot(columns_in, gate_local, preferred_element_type=jnp.float32)
    up_sum = jnp.dot(columns_in, up_local, preferred_element_type=jnp.float32)
    hidden = (jax.nn.silu(gate_sum) * up_sum).astype(jnp.bfloat16)
    partial_out = jnp.dot(hidden, down_local, preferred_element_type=jnp.float32).astype(
        jnp.bfloat16
    )
    finished = (
        lax.psum_scatter(partial_out, "etp", scatter_dimension=1, tiled=True)
        .astype(jnp.float32)
        .astype(jnp.bfloat16)
    )
    results = lax.all_to_all(
        finished.reshape(cycle_size, CAP, local_width),
        "expert",
        split_axis=0,
        concat_axis=0,
        tiled=True,
    )
    flat_results = results.reshape(slot_total, local_width).astype(jnp.float32)
    mixed = jnp.dot(combine_table, flat_results, precision=lax.Precision.HIGHEST)
    return mixed.astype(jnp.bfloat16)


FOUR = 4
HALVES = 2
RING_IN = 5
RING_OUT = 3
BLOCK = 256
EARLY = 2
WIDE = 4
READY = (0, 0, 1, 2, 3, 5, 6, 7)
RELAY = 3
TARGETS = (0, 1, 0, 1, 0, 1, 0, 1, 2, 2, 2, 2, 3, 3, 3, 3)


def partner(me, step):
    low = (me % 2 + step % 2) % 2
    high = (me // 2 + step // 2) % 2
    return low + 2 * high


def layer_kernel(
    tok_hbm, route_hbm, weight_hbm, gate_hbm, up_hbm, down_hbm, out_ref,
    routes, weights, toks, chosen, pick, comb, acc_gate, acc_up, hidden,
    ring_in, ring_out, kept, core_out, core_in, x_out, x_in, z_out, z_in,
    sem_in, sem_out, sem_own, sem_sent, meta_r, z_r, x_r, ca_r, cb_r, rc_r, rx_r, rz_r,
):
    rows, width = tok_hbm.shape
    inner = gate_hbm.shape[2]
    e = lax.axis_index("expert")
    z = lax.axis_index("etp")
    middle = (z + 1) // 2 % 2
    sub = width // HALVES
    tile = inner // HALVES
    subs = FOUR * HALVES
    steps_in = subs * HALVES
    units = len(TARGETS)
    slabs = units // 2
    rank = [TARGETS[:i].count(TARGETS[i]) for i in range(units)]
    place = {(TARGETS[i], rank[i]): i for i in range(units)}

    def origin(p):
        return partner(z, p + middle * (p // 2) * (1 - 2 * (p % 2)))

    def fetch_in(t, slot):
        k = t // HALVES
        row = pl.multiple_of(origin(k // HALVES) * width + k % HALVES * sub, sub)
        col = pl.multiple_of(t % HALVES * tile, tile)
        return [
            pltpu.make_async_copy(
                hbm.at[0, pl.ds(row, sub), pl.ds(col, tile)],
                ring_in.at[slot, :, pl.ds(m * tile, tile)],
                sem_in.at[slot],
            )
            for m, hbm in enumerate((gate_hbm, up_hbm))
        ]

    def await_in(slot):
        pltpu.make_async_copy(
            gate_hbm.at[0, pl.ds(0, sub), :], ring_in.at[slot], sem_in.at[slot]
        ).wait()

    def await_out(u):
        pltpu.make_async_copy(
            down_hbm.at[0, :, pl.ds(0, 2 * BLOCK)], ring_out.at[u % RING_OUT],
            sem_out.at[u % RING_OUT],
        ).wait()

    def step_of(target):
        return FOUR - 1 - target + middle * (target * (2 - target) * 2 - 1) * (target < 2)

    def fetch_out(u):
        return [
            pltpu.make_async_copy(
                down_hbm.at[0, :, pl.ds(
                    pl.multiple_of(
                        partner(z, step_of(TARGETS[i])) * width + rank[i] * BLOCK, BLOCK
                    ), BLOCK
                )],
                ring_out.at[u % RING_OUT, :, pl.ds(i % 2 * BLOCK, BLOCK)],
                sem_out.at[u % RING_OUT],
            )
            for i in (2 * u, 2 * u + 1)
        ]

    def send(source, target, kind, r_sem, axis, step):
        me = e if axis == "expert" else z
        return pltpu.make_async_remote_copy(
            src_ref=source, dst_ref=target, send_sem=sem_sent.at[kind], recv_sem=r_sem,
            device_id={axis: partner(me, step)},
            device_id_type=pl.DeviceIdType.MESH,
        )

    barrier = pltpu.get_barrier_semaphore()

    def greet(axis, me, step):
        pl.semaphore_signal(
            barrier, inc=1, device_id={axis: partner(me, step)},
            device_id_type=pl.DeviceIdType.MESH,
        )

    greet("etp", z, 2)
    pl.when(middle == 1)(lambda: greet("etp", z, 3))
    greet("etp", z, 1)
    for step in (3, 2, 1):
        greet("expert", e, step)

    own = [
        pltpu.make_async_copy(route_hbm, routes.at[0], sem_own.at[0]),
        pltpu.make_async_copy(weight_hbm, weights.at[0], sem_own.at[1]),
    ] + [
        pltpu.make_async_copy(
            tok_hbm.at[:, pl.ds(h * sub, sub)], toks.at[0, 0, h], sem_own.at[2 + h]
        )
        for h in range(HALVES)
    ]
    for copy in own:
        copy.start()
    for copy in own:
        copy.wait()
    for t in range(RING_IN):
        for copy in fetch_in(t, t):
            copy.start()

    earlier = (
        lax.broadcasted_iota(jnp.int32, (rows, rows), 0)
        < lax.broadcasted_iota(jnp.int32, (rows, rows), 1)
    ).astype(jnp.bfloat16)
    slot_row = lax.broadcasted_iota(jnp.int32, (rows, rows), 0).astype(jnp.float32)

    def place_block(j):
        route, weigh = routes[j], weights[j]
        first = route[0:1, :] == e
        second = route[1:2, :] == e
        routed = jnp.where(first, 1.0, 0.0) + jnp.where(second, 1.0, 0.0)
        weight = jnp.where(first, weigh[0:1, :], 0.0) + jnp.where(second, weigh[1:2, :], 0.0)
        slot = jnp.dot(
            jnp.broadcast_to(routed, (16, rows)).astype(jnp.bfloat16), earlier,
            preferred_element_type=jnp.float32,
        )[0:1, :]
        slot = jnp.where(routed > 0.5, slot, -1.0)
        hit = slot_row == slot
        pick[j] = jnp.where(hit, 1.0, 0.0).astype(jnp.bfloat16)
        comb[j] = jnp.where(hit, weight, 0.0).T.astype(jnp.bfloat16)

    place_block(0)
    pl.semaphore_wait(barrier, FOUR + 1 + middle)

    meta_copies = {
        j: [
            send(held.at[0], held.at[j], m, meta_r.at[m, j], "expert", j)
            for m, held in enumerate((routes, weights))
        ]
        for j in (2, 3, 1)
    }
    near_copies = [
        send(toks.at[0, 0, h], toks.at[1, 0, h], 2, z_r.at[1, h], "etp", 1)
        for h in range(HALVES)
    ]
    far_copies = [
        send(
            toks.at[0, 0, h], toks.at[3 - middle, 0, h], 2,
            z_r.at[3 - middle, h], "etp", 2 + middle,
        )
        for h in range(HALVES)
    ]
    z_copies, forward, x_copies, ca_copies, cb_copies = [], [], [], [], []
    for k in range(subs):
        p, h = k // HALVES, k % HALVES
        mine = toks.at[p, 0, h]
        z_copies.append(send(mine, mine, 3, z_r.at[p, h], "etp", 1))
        x_copies.append(
            send(mine, toks.at[p, 2, h], 4, x_r.at[k], "expert", 2)
        )
        ca_copies.append(
            send(mine, toks.at[p, 1, h], 5, ca_r.at[k], "expert", 1)
        )
        cb_copies.append(
            send(toks.at[p, 2, h], toks.at[p, 3, h], 6, cb_r.at[k], "expert", 1)
        )
    for pair in meta_copies.values():
        for copy in pair:
            copy.start()
    for h in range(HALVES):
        ca_copies[h].start()
        x_copies[h].start()
        near_copies[h].start()

    def send_far():
        for copy in far_copies:
            copy.start()

    pl.when(middle == 1)(send_far)

    def place_from(j):
        for copy in meta_copies[j]:
            copy.wait_recv()
        place_block(j)

    def pass_over(k):
        if k < subs:
            x_copies[k].wait_recv()
            cb_copies[k].start()

    def pass_on(k):
        if k < subs:
            if k < 2 * HALVES:
                z_copies[k].wait_recv()
            else:
                pl.when(middle == 0)(z_copies[k].wait_recv)
            x_copies[k].start()
            ca_copies[k].start()

    def pass_out(k):
        if k < subs:

            @pl.when(middle == 1)
            def _():
                z_copies[k].wait_recv()
                z_copies[k].start()

    def poll(k):
        pass_over(k)
        pass_out(k + 2 * HALVES)
        pass_on(k + HALVES)

    def select(k, first, stop):
        for j in range(first, stop):
            chosen[k % 2, pl.ds(j * CAP, CAP), :] = jnp.dot(
                pick[j, 0:CAP, :], toks[k // HALVES, j, k % HALVES],
                preferred_element_type=jnp.float32,
            ).astype(jnp.bfloat16)

    def multiply(k, first, stop, fresh, release):
        span = slice(first * CAP, stop * CAP)

        def tile_step(n):
            t = k * HALVES + n
            slot = lax.rem(t, RING_IN)
            start = n * tile
            col = pl.ds(start if isinstance(n, int) else pl.multiple_of(start, tile), tile)
            both = jnp.dot(
                chosen[k % 2, span, :], ring_in[slot], preferred_element_type=jnp.float32
            )
            gate, up = both[:, :tile], both[:, tile:]
            if k > 0:
                gate = gate + acc_gate[span, col]
                up = up + acc_up[span, col]
            if k < subs - 1:
                acc_gate[span, col] = gate
                acc_up[span, col] = up
            else:
                hidden[span, col] = (gate * (0.5 * jnp.tanh(0.5 * gate) + 0.5) * up).astype(jnp.bfloat16)

        def refill(n):
            t = k * HALVES + n
            slot = lax.rem(t, RING_IN)

            @pl.when(t + RING_IN < steps_in)
            def _():
                for copy in fetch_in(t + RING_IN, slot):
                    copy.start()

        def in_step(n, carry):
            if release and k + 1 < subs:
                pl.when(n == 1)(functools.partial(poll, k + 1))
            if fresh:
                await_in(lax.rem(k * HALVES + n, RING_IN))
            tile_step(n)
            if release:
                refill(n)
            return carry

        if k < WIDE:
            lax.fori_loop(0, HALVES, in_step, 0)
        else:
            if k + 1 < subs:
                poll(k + 1)
            for n in range(HALVES):
                await_in((k * HALVES + n) % RING_IN)
            for n in range(HALVES):
                tile_step(n)
            for n in range(HALVES):
                refill(n)

    place_from(1)
    for k in range(EARLY):
        ca_copies[k].wait_recv()
        select(k, 0, 2)
        multiply(k, 0, 2, True, False)
    place_from(2)
    place_from(3)
    poll(0)
    pl.when(middle == 0)(send_far)
    for k in range(EARLY):
        cb_copies[k].wait_recv()
        select(k, 2, FOUR)
        multiply(k, 2, FOUR, False, True)
    for k in range(EARLY, subs):
        ca_copies[k].wait_recv()
        cb_copies[k].wait_recv()
        select(k, 0, FOUR)
        if subs - 1 - k < RING_OUT:
            for copy in fetch_out(k - subs + RING_OUT):
                copy.start()
        multiply(k, 0, FOUR, True, True)

    core_copies = [
        [
            send(
                core_out.at[part, pl.ds(2 * u, 2)], core_in.at[part, pl.ds(2 * u, 2)],
                7, rc_r.at[part, u], "expert", 1,
            )
            for u in range(slabs)
        ]
        for part in range(2)
    ]
    rx_copies = [
        send(x_out.at[i], x_in.at[i], 8, rx_r.at[i], "expert", 2)
        for i in range(units)
    ]
    own_at = place[FOUR - 1, 0]
    rz_copies = []
    for i in range(own_at):
        target = TARGETS[i]
        at = i if target == 2 else i + middle * (own_at + rank[i] - i)
        step = 1 if target == 2 else 1 + middle * (1 + target)
        rz_copies.append(send(z_out.at[i], z_in.at[at], 9, rz_r.at[at], "etp", step))
    landings = [
        send(z_out.at[i], z_in.at[i], 9, rz_r.at[i], "etp", 1) for i in range(units)
    ]

    def x_stage(u):
        core_copies[1][u].wait_recv()
        for i in (2 * u, 2 * u + 1):
            x_out[i] = (kept[i, 1] + core_in[1, i].astype(jnp.float32)).astype(jnp.bfloat16)
            rx_copies[i].start()

    def z_sum(i):
        if i % 2 == 0:
            core_copies[0][i // 2].wait_recv()
        rx_copies[i].wait_recv()
        return kept[i, 0] + core_in[0, i].astype(jnp.float32) + x_in[i].astype(jnp.float32)

    def z_send(i):
        z_out[i] = z_sum(i).astype(jnp.bfloat16)
        rz_copies[i].start()

    def z_relay(i):
        both = z_sum(i)
        landings[i].wait_recv()
        z_out[i] = (both + z_in[i].astype(jnp.float32)).astype(jnp.bfloat16)
        rz_copies[i].start()

    def z_stage(i):
        if i < units:
            if TARGETS[i] < 2:
                pl.when(middle == 0)(functools.partial(z_send, i))
            elif TARGETS[i] == 2:
                z_send(i)
            else:
                both = z_sum(i)
                for at in (place[2, rank[i]], own_at + rank[i]):
                    landings[at].wait_recv()
                    both = both + z_in[at].astype(jnp.float32)
                col = rank[i] * BLOCK
                out_ref[:, col:col + BLOCK] = both.astype(jnp.bfloat16)
        if i >= RELAY and TARGETS[i - RELAY] < 2:
            pl.when(middle == 1)(functools.partial(z_relay, i - RELAY))

    def project(u, first, stop):
        part = jnp.dot(
            hidden[first * CAP:stop * CAP, :], ring_out[u % RING_OUT],
            preferred_element_type=jnp.float32,
        ).astype(jnp.bfloat16)
        for j in range(first, stop):
            share = jnp.dot(
                comb[j, :, 0:CAP], part[(j - first) * CAP:(j - first + 1) * CAP, :],
                preferred_element_type=jnp.float32,
            )
            for m in range(2):
                piece = share[:, m * BLOCK:(m + 1) * BLOCK]
                if j % 2 == 0:
                    kept[2 * u + m, j // 2] = piece
                else:
                    core_out[j // 2, 2 * u + m] = piece.astype(jnp.bfloat16)
        for half in range(stop // 2 - 1, first // 2 - 1, -1):
            core_copies[half][u].start()
        if first == 0 and u + RING_OUT < slabs:
            for copy in fetch_out(u + RING_OUT):
                copy.start()

    for u in range(EARLY):
        await_out(u)
        project(u, 2, FOUR)
    for u in range(EARLY):
        x_stage(u)
        project(u, 0, 2)
    done = 0
    for u in range(EARLY, slabs):
        await_out(u)
        project(u, 0, FOUR)
        if u > EARLY:
            x_stage(u - 1)
        for i in range(done, READY[u]):
            z_stage(i)
        done = READY[u]
    x_stage(slabs - 1)

    def drain(kind, source):
        send(source, source, kind, sem_sent.at[kind], "expert", 1).wait_send()

    drain(0, routes.at[pl.ds(0, FOUR - 1)])
    drain(1, weights.at[pl.ds(0, FOUR - 1)])
    drain(2, toks.at[0, pl.ds(0, 2)])
    pl.when(middle == 1)(lambda: drain(3, toks.at[0, pl.ds(0, 2)]))
    for kind in (4, 5, 6):
        drain(kind, toks.at[0])
    for i in range(done, units):
        z_stage(i)
    drain(7, core_out)
    drain(8, x_out)
    drain(9, z_out.at[pl.ds(0, own_at)])


def fused(tokens, route_ids, gate_weights, w_gate, w_up, w_down):
    rows, width = tokens.shape
    inner = w_gate.shape[2]
    slots = FOUR * CAP
    units, subs = len(TARGETS), FOUR * HALVES
    bf, f32 = jnp.bfloat16, jnp.float32
    dma = pltpu.SemaphoreType.DMA
    hbm = pl.BlockSpec(memory_space=pl.ANY)
    return pl.pallas_call(
        layer_kernel,
        out_shape=pltpu.VMEM((rows, width), bf),
        in_specs=[hbm] * 6,
        out_specs=pl.BlockSpec(memory_space=pltpu.VMEM),
        scratch_shapes=[
            pltpu.VMEM((FOUR, 2, rows), jnp.int32),
            pltpu.VMEM((FOUR, 2, rows), f32),
            pltpu.VMEM((FOUR, FOUR, HALVES, rows, width // HALVES), bf),
            pltpu.VMEM((2, slots, width // HALVES), bf),
            pltpu.VMEM((FOUR, rows, rows), bf),
            pltpu.VMEM((FOUR, rows, rows), bf),
            pltpu.VMEM((slots, inner), f32),
            pltpu.VMEM((slots, inner), f32),
            pltpu.VMEM((slots, inner), bf),
            pltpu.VMEM((RING_IN, width // HALVES, inner), bf),
            pltpu.VMEM((RING_OUT, inner, 2 * BLOCK), bf),
            pltpu.VMEM((units, 2, rows, BLOCK), f32),
            pltpu.VMEM((2, units, rows, BLOCK), bf),
            pltpu.VMEM((2, units, rows, BLOCK), bf),
            pltpu.VMEM((units, rows, BLOCK), bf),
            pltpu.VMEM((units, rows, BLOCK), bf),
            pltpu.VMEM((units, rows, BLOCK), bf),
            pltpu.VMEM((units, rows, BLOCK), bf),
            dma((RING_IN,)), dma((RING_OUT,)), dma((2 + HALVES,)), dma((10,)),
            dma((2, FOUR)), dma((FOUR, HALVES)), dma((subs,)), dma((subs,)), dma((subs,)),
            dma((2, units // 2)), dma((units,)), dma((units,)),
        ],
        compiler_params=pltpu.CompilerParams(
            collective_id=0, has_side_effects=True, vmem_limit_bytes=66500000
        ),
    )(tokens, route_ids.T, gate_weights.T, w_gate, w_up, w_down)


def pick_body(tokens, route_ids, gate_weights, w_gate, w_up, w_down):
    square = lax.axis_size("expert") == FOUR and lax.axis_size("etp") == FOUR
    whole = tokens.shape == (128, len(TARGETS) * BLOCK // FOUR)
    lanes = w_gate.shape[2] % (HALVES * 128) == 0
    body = fused if square and whole and lanes else shards
    return body(tokens, route_ids, gate_weights, w_gate, w_up, w_down)


def solution(mesh):
    return jax.shard_map(
        pick_body,
        mesh=mesh,
        in_specs=(
            P(("groups", "expert"), "etp"),
            P(("groups", "expert"), None),
            P(("groups", "expert"), None),
            P("expert", None, "etp"),
            P("expert", None, "etp"),
            P("expert", "etp", None),
        ),
        out_specs=P(("groups", "expert"), "etp"),
        check_vma=False,
    )
```

time: 75.3 us -> 67.6 us (0.90)
  Pallas kernels: 72.8 us -> 66.7 us
  local copies, waits for them, and re-layouts: 1.67 us -> 0.71 us
    pallas_call x1, Pallas kernels: 72.8 us -> 66.7 us  [fused(): pl.pallas_call(layer_kernel, out_shape=pltpu.VMEM((rows, width), bf), in_...]
    unnamed x1, local copies, waits for them, and re-layouts: 1.67 us -> 0.71 us
where the time goes in v2:
time: 67.6 us; the launch traced here: 67.4 us
  Pallas kernels  66.7 us (99%)
  local copies, waits for them, and re-layouts  0.71 us (1%)
    pallas_call x1, Pallas kernels, fused(): pl.pallas_call(layer_kernel, out_shape=pltpu.VMEM((rows, width), bf), in_...  66.7 us

profile of v2, /device:TPU:0, one launch (start us, length us, event | category | flops | bytes accessed | tf_op | source)
XLA Modules:
  0.0 67.4 jit_solution(14853850134641898693)
XLA Ops:
  0.0 66.7 %shard_map.64 = bf16[128,1024]{1,0:T(8,128)(2,1)S(1)} custom-call(bf16[128,1024]{1,0:T(8,128)(2,1)} %tok_hbm.1, s32[2,128]{1,0:T(2,128)} %bitcast.2, f32[2,128]{1,0:T(2,128)} %bitcast.3, bf16[1,4096,3584]{2,1,0:T(8,128)(2,1)} %gate_hbm.1, bf16[1,4096,3584]{2,1,0:T(8,128)(2,1)} %up_hbm.1, bf16[1,3584,4096]{2,1,0:T(8,128)(2,1)} %down_hbm.1), custom_call_target="tpu_custom_call" | custom-call | tf_op jit(solution)/shard_map/pallas_call | solution.py:490
  66.7 0.7 %copy.8 = bf16[128,1024]{1,0:T(8,128)(2,1)} copy(bf16[128,1024]{1,0:T(8,128)(2,1)S(1)} %shard_map.64) | data formatting | bytes 524288
